TPU v7x, 256 devices: a whole 4x4x8 slice. The times are simulated.
256 devices in a mesh: rows: 32 (over y, z), cols: 8 (over x, core).
Axes of the slice: x: 4, y: 4, z: 8, core: 2. Of those that a mesh axis runs over, the one named last changes fastest.
Arguments:
- token_ids: int32 [128, 256], P('rows'), may hold values from 0 to 8191
- keep_mask: int32 [128, 256], P('rows'), may hold values 0 or 1
- remask_order: int32 [32768], P('rows'), may hold values from 0 to 32767, each once
- embed_table: bfloat16 [8192, 1024], P(None, 'cols'), may hold values from -6 to 6
- mask_embed: bfloat16 [1024], P('cols'), may hold values from -4 to 4
- conv_one: bfloat16 [3, 3, 1024, 1024], P(None, None, None, 'cols'), may hold values from -0.0625 to 0.0625
- gain_one: float32 [1024], P('cols'), may hold values from 0.25 to 1.75
- bias_one: float32 [1024], P('cols'), may hold values from -3 to 3
- conv_two: bfloat16 [3, 3, 1024, 1024], P(None, None, None, 'cols'), may hold values from -0.0625 to 0.0625
- gain_two: float32 [1024], P('cols'), may hold values from 0.25 to 1.75
- bias_two: float32 [1024], P('cols'), may hold values from -3 to 3
- head_weight: bfloat16 [1024, 8192], P(None, 'cols'), may hold values from -15.6 to 15.6
Outputs:
- features: bfloat16 [128, 256, 1024], P('rows', None, 'cols')
- token_logp: float32 [128, 256], P('rows', 'cols')
Inputs may be any that keep to these rules, and one draw needn't show every extreme that they name: `remask_order`: each rank appears once.
All inputs are finite; a program needn't handle non-finite values. No bound on the sum of `keep_mask` on one device may be relied on, other than what follows from the above.
Results may differ from a plain program's by a relative error of at most 0.0039.
Values may be sent and summed in bfloat16 or wider, within the bound.
A program may use at most 128 MiB of HBM per device.

v0:
```python
import jax
import jax.numpy as jnp
from jax import lax
from jax.sharding import PartitionSpec as P

C = 1024
GROUPS = 32


def with_halo(value, sides, width):
    for axis, dim in sides:
        count, length = (lax.axis_size(axis), value.shape[dim])
        up = [(i, (i + 1) % count) for i in range(count - 1)]
        down = [(j, i) for i, j in up]
        last = lax.slice_in_dim(value, length - width, length, axis=dim)
        leading = lax.slice_in_dim(value, 0, width, axis=dim)
        before = lax.ppermute(last, axis, up)
        after = lax.ppermute(leading, axis, down)
        value = jnp.concatenate([before, value, after], axis=dim)
    return value


def sent_to_all(value, axis):
    copies = jnp.broadcast_to(value, (lax.axis_size(axis), *value.shape))
    return lax.all_to_all(copies, axis, split_axis=0, concat_axis=0, tiled=True)


def over_copies(value, axis):
    return sent_to_all(value, axis).sum(axis=0)


def together(arrays, axis):
    ends = [0]
    for a in arrays:
        ends.append(ends[-1] + a.size)
    so_far = over_copies(jnp.concatenate([a.ravel() for a in arrays]), axis)
    return tuple((so_far[b:e].reshape(a.shape) for a, b, e in zip(arrays, ends, ends[1:])))


def laid_out(tiles, dim):
    tiles = jnp.moveaxis(tiles, 0, dim)
    lengths = tiles.shape
    return tiles.reshape(*lengths[:dim], lengths[dim] * lengths[dim + 1], *lengths[dim + 2 :])


def gathered_copies(value, axis, dim):
    tiles = sent_to_all(value, axis)
    return laid_out(tiles, dim)


def all_in_one(value, axis):
    leaves = jax.tree.leaves(value)
    order = sorted(range(len(leaves)), key=lambda k: -leaves[k].size)
    width = (1, *leaves[order[0]].shape)[-1]
    lines = [
        jnp.pad(leaves[k].reshape(-1), (0, -leaves[k].size % width)).reshape(-1, width)
        for k in order
    ]
    both, at, found = (sent_to_all(jnp.concatenate(lines), axis), 0, {})
    for k, line in zip(order, lines):
        section = both[:, at : at + len(line)].reshape(len(both), -1)
        found[k] = section[:, : leaves[k].size].reshape(-1, *leaves[k].shape)
        at += len(line)
    numbers = iter(range(len(leaves)))
    return jax.tree.map(lambda _: found[next(numbers)], value)


def folded_in_pairs(pieces, combine):
    while len(jax.tree.leaves(pieces)[0]) > 1:
        pieces = jax.vmap(combine)(
            *(jax.tree.map(lambda part: part[side::2], pieces) for side in (0, 1))
        )
    return jax.tree.map(lambda part: part[0], pieces)


def joined_all(value, axis, combine):
    pieces = all_in_one(value, axis)
    return folded_in_pairs(pieces, combine)


def add_taps(total, weight, piece):
    rows_here = piece.shape[0] - 2
    width = piece.shape[1]
    count = piece.shape[2]
    padded = jnp.pad(piece, ((0, 0), (1, 1), (0, 0)))
    for shift_row in range(3):
        for shift_col in range(3):
            window = padded[
                shift_row : shift_row + rows_here, shift_col : shift_col + width
            ].reshape(-1, count)
            taps = weight[shift_row, shift_col]
            total = total + jnp.dot(window, taps, preferred_element_type=jnp.float32)
    return total


def convolve(field, weight):
    rows_here, width, _ = field.shape
    empty = jnp.zeros((rows_here * width, weight.shape[3]), jnp.float32)
    rimmed = with_halo(field, (("rows", 0),), 1)
    total = add_taps(empty, weight, lax.all_gather(rimmed, "cols", axis=2, tiled=True))
    return total.reshape(rows_here, width, -1)


def group_norm(values, gain, bias, height):
    rows_here, width, channels = values.shape
    group_width = C // GROUPS
    flat = values.reshape(rows_here * width, channels // group_width, group_width)
    population = height * width * group_width
    sums, squares = together(
        (jnp.sum(flat, axis=(0, 2)), jnp.sum(flat * flat, axis=(0, 2))), "rows"
    )
    mean = sums / population
    variance = squares / population - mean * mean
    deviation = flat - mean[None, :, None]
    normed = deviation / jnp.sqrt(variance + 1e-05)[None, :, None]
    return normed.reshape(rows_here, width, channels) * gain + bias


def combine_totals(first, second):
    top = jnp.maximum(first[0], second[0])
    summed = first[1] * jnp.exp(first[0] - top) + second[1] * jnp.exp(second[0] - top)
    return (top, summed, first[2] + second[2])


def local(
    token_ids,
    keep_mask,
    remask_order,
    embed_table,
    mask_embed,
    conv_one,
    gain_one,
    bias_one,
    conv_two,
    gain_two,
    bias_two,
    head_weight,
):
    rows_here, width = token_ids.shape
    height = rows_here * lax.axis_size("rows")
    num_cols = lax.axis_size("cols")
    order = remask_order.reshape(rows_here, width)
    visible = (keep_mask == 1) | (order >= height * width // 2)
    looked = jnp.take(embed_table, token_ids, axis=0)
    start = jnp.where(visible[:, :, None], looked, mask_embed[None, None, :])
    hidden = jax.nn.silu(group_norm(convolve(start, conv_one), gain_one, bias_one, height)).astype(
        jnp.bfloat16
    )
    second = group_norm(convolve(hidden, conv_two), gain_two, bias_two, height)
    features = (start.astype(jnp.float32) + second).astype(jnp.bfloat16)
    vocab_here = head_weight.shape[1]
    piece = gathered_copies(features, "cols", 2)
    count = piece.shape[2]
    logits = jnp.dot(piece.reshape(-1, count), head_weight, preferred_element_type=jnp.float32)
    top = jnp.max(logits, axis=1)
    summed = jnp.sum(jnp.exp(logits - top[:, None]), axis=1)
    offset = lax.axis_index("cols") * vocab_here
    vocab_ids = lax.broadcasted_iota(jnp.int32, (1, vocab_here), 1) + offset
    hits = vocab_ids == token_ids.reshape(-1, 1)
    picked = jnp.sum(jnp.where(hits, logits, 0.0), axis=1)
    top, summed, picked = joined_all((top, summed, picked), "cols", combine_totals)
    logp = (picked - top - jnp.log(summed)).reshape(rows_here, width)
    slice_width = width // num_cols
    token_logp = lax.dynamic_slice_in_dim(
        logp, lax.axis_index("cols") * slice_width, slice_width, 1
    )
    return (features, token_logp)


def solution(mesh):
    in_specs = (
        P("rows", None),
        P("rows", None),
        P("rows"),
        P(None, "cols"),
        P("cols"),
        P(None, None, None, "cols"),
        P("cols"),
        P("cols"),
        P(None, None, None, "cols"),
        P("cols"),
        P("cols"),
        P(None, "cols"),
    )
    out_specs = (P("rows", None, "cols"), P("rows", "cols"))
    return jax.shard_map(local, mesh=mesh, in_specs=in_specs, out_specs=out_specs, check_vma=False)
```

profile of v0, /device:TPU:1, one launch (start us, length us, event | category | flops | bytes accessed | tf_op | source)
XLA Modules:
  0.0 250.8 jit_solution(9500933285625379632)
XLA Ops:
  9.5 4.7 %gather_fusion = bf16[1024,128]{1,0:T(8,128)(2,1)S(1)} fusion(bf16[8192,128]{1,0:T(8,128)(2,1)} %param.15, s32[1024]{0:T(1024)S(1)} %broadcast_clamp_fusion), kind=kCustom, calls=%fused_computation | custom fusion | bytes 528384 | tf_op jit(solution)/shard_map/jit(_take)/gather | solution.py:144
  14.6 4.4 %collective-permute-start = (bf16[1,256,128]{2,1,0:T(8,128)(2,1)S(1)}, bf16[1,256,128]{2,1,0:T(8,128)(2,1)S(1)}, u32[]{:S(2)}, u32[]{:S(2)}) collective-permute-start(bf16[1,256,128]{2,1,0:T(8,128)(2,1)S(1)} %get-tuple-element.32), channel_id=1, source_target_pairs={{0,8},{8,16},{16,24},{24,32},{32,40},{40,48},{48,56},{56,64},{64,7... | collective-permute-start | bytes 196616 | tf_op jit(solution)/shard_map/ppermute | solution.py:17
  20.3 3.9 %collective-permute-done.1 = bf16[1,256,128]{2,1,0:T(8,128)(2,1)S(1)} collective-permute-done((bf16[1,256,128]{2,1,0:T(8,128)(2,1)S(1)}, bf16[1,256,128]{2,1,0:T(8,128)(2,1)S(1)}, u32[]{:S(2)}, u32[]{:S(2)}) %collective-permute-start.1) | collective-permute-done | bytes 65568 | tf_op jit(solution)/shard_map/ppermute | solution.py:18
  25.0 38.2 %all-gather.3.cloned.1.call-done = bf16[6,256,1024]{2,1,0:T(8,128)(2,1)} async-done(((bf16[6,256,128]{2,1,0:T(8,128)(2,1)}), bf16[6,256,1024]{2,1,0:T(8,128)(2,1)}) %all-gather.3.cloned.1.call-update) | async-done | bytes 3145744 | tf_op jit(solution)/shard_map/all_gather | solution.py:100
  63.3 13.0 %pad_slice_fusion.6 = (bf16[4,256,1024]{2,1,0:T(8,128)(2,1)S(1)}, bf16[4,256,1024]{2,1,0:T(8,128)(2,1)}, bf16[4,256,1024]{2,1,0:T(8,128)(2,1)}, bf16[4,256,1024]...) fusion(bf16[6,256,1024]{2,1,0:T(8,128)(2,1)} %all-gather.3.clon, ...), kind=kLoop, calls=%fused_computation.12 | loop fusion | bytes 28311552 | tf_op jit(solution)/shard_map/slice | solution.py:88
  76.3 1.8 fusion.21
  78.1 1.8 convolution_add_fusion.15
  79.9 1.8 convolution_add_fusion.14
  86.8 18.0 %all_to_all.22 = f32[32,1,8]{2,1,0:T(1,128)S(1)} all-to-all(f32[32,1,8]{2,1,0:T(1,128)S(1)} %broadcast_in_dim.60), channel_id=1, replica_groups=mesh['rows'=32,'cols'=8] {'rows'}, dimensions={0} | all-to-all | bytes 2048 | tf_op jit(solution)/shard_map/all_to_all | solution.py:25
  105.5 2.2 collective-permute-start.2
  109.2 3.5 %collective-permute-done.3 = bf16[1,256,128]{2,1,0:T(8,128)(2,1)S(1)} collective-permute-done((bf16[1,256,128]{2,1,0:T(8,128)(2,1)S(1)}, bf16[1,256,128]{2,1,0:T(8,128)(2,1)S(1)}, u32[]{:S(2)}, u32[]{:S(2)}) %collective-permute-start.3) | collective-permute-done | bytes 65568 | tf_op jit(solution)/shard_map/ppermute | solution.py:18
  113.5 35.7 %all-gather.5.cloned.1.call-done = bf16[6,256,1024]{2,1,0:T(8,128)(2,1)} async-done(((bf16[6,256,128]{2,1,0:T(8,128)(2,1)}), bf16[6,256,1024]{2,1,0:T(8,128)(2,1)}) %all-gather.5.cloned.1.call-update) | async-done | bytes 3145744 | tf_op jit(solution)/shard_map/all_gather | solution.py:100
  149.2 13.0 %pad_slice_fusion = (bf16[4,256,1024]{2,1,0:T(8,128)(2,1)S(1)}, bf16[4,256,1024]{2,1,0:T(8,128)(2,1)}, bf16[4,256,1024]{2,1,0:T(8,128)(2,1)}, bf16[4,256,1024]{2...) fusion(bf16[6,256,1024]{2,1,0:T(8,128)(2,1)} %all-gather.5.clon, ...), kind=kLoop, calls=%fused_computation.6 | loop fusion | bytes 28311552 | tf_op jit(solution)/shard_map/slice | solution.py:88
  162.2 1.8 fusion.11
  164.0 1.8 convolution_add_fusion.7
  165.9 1.8 convolution_add_fusion.6
  172.7 18.0 %all_to_all.23 = f32[32,1,8]{2,1,0:T(1,128)S(1)} all-to-all(f32[32,1,8]{2,1,0:T(1,128)S(1)} %broadcast_in_dim.61), channel_id=1, replica_groups=mesh['rows'=32,'cols'=8] {'rows'}, dimensions={0} | all-to-all | bytes 2048 | tf_op jit(solution)/shard_map/all_to_all | solution.py:25
  191.6 1.8 broadcast_in_dim.62
  193.3 6.0 %all-to-all-start.2 = ((bf16[8,4,256,128]{3,2,1,0:T(8,128)(2,1)}), bf16[8,4,256,128]{3,2,1,0:T(8,128)(2,1)}, u32[]{:S(2)}, u32[]{:S(2)}) async-start(bf16[8,4,256,128]{3,2,1,0:T(8,128)(2,1)} %broadcast_in_dim.62), calls=%async_computation.2 | async-start | bytes 4194304 | tf_op jit(solution)/shard_map/all_to_all | solution.py:25
  199.4 26.3 %all-to-all-done.2 = bf16[8,4,256,128]{3,2,1,0:T(8,128)(2,1)} async-done(((bf16[8,4,256,128]{3,2,1,0:T(8,128)(2,1)}), bf16[8,4,256,128]{3,2,1,0:T(8,128)(2,1)}, u32[]{:S(2)}, u32[]{:S(2)}) %all-to-all-start.2) | async-done | bytes 2097184 | tf_op jit(solution)/shard_map/all_to_all | solution.py:25
  225.7 2.9 %copy.22 = bf16[4,256,8,128]{3,2,1,0:T(8,128)(2,1)S(1)} copy(bf16[4,256,8,128]{3,1,0,2:T(8,128)(2,1)} %bitcast.39) | data formatting | bytes 4194304 | tf_op jit(solution)/shard_map/transpose | solution.py:41
  228.7 2.4 fusion.52
  233.2 4.2 %all-to-all-start.3 = ((f32[8,3,1024]{2,1,0:T(4,128)}), f32[8,3,1024]{2,1,0:T(4,128)S(1)}, u32[]{:S(2)}, u32[]{:S(2)}) async-start(f32[8,3,1024]{2,1,0:T(4,128)} %broadcast_in_dim.64), calls=%async_computation.3 | async-start | bytes 262144 | tf_op jit(solution)/shard_map/all_to_all | solution.py:25
  237.4 5.3 %all-to-all-done.3 = f32[8,3,1024]{2,1,0:T(4,128)S(1)} async-done(((f32[8,3,1024]{2,1,0:T(4,128)}), f32[8,3,1024]{2,1,0:T(4,128)S(1)}, u32[]{:S(2)}, u32[]{:S(2)}) %all-to-all-start.3) | async-done | bytes 98336 | tf_op jit(solution)/shard_map/all_to_all | solution.py:25
  (117 shorter events, 21.7 us)
Async XLA Ops:
  7.2 221.5 %copy-start = (bf16[1024,1024]{1,0:T(8,128)(2,1)S(1)}, bf16[1024,1024]{1,0:T(8,128)(2,1)}, u32[]{:S(2)}) copy-start(bf16[1024,1024]{1,0:T(8,128)(2,1)} %param.23) | copy-start | bytes 6291460
  7.2 7.1 %copy-start.11 = (bf16[128]{0:T(256)(128)(2,1)S(1)}, bf16[128]{0:T(256)(128)(2,1)}, u32[]{:S(2)}) copy-start(bf16[128]{0:T(256)(128)(2,1)} %param.16) | copy-start | bytes 772
  7.2 56.1 %all-gather.3.cloned.1.call-start = ((), (), s32[]{:S(2)}) async-start(), calls=%async_computation.4 | async-start | bytes 3538944 | tf_op jit(solution)/shard_map/all_gather | solution.py:100
  14.6 5.7 %collective-permute-start = (bf16[1,256,128]{2,1,0:T(8,128)(2,1)S(1)}, bf16[1,256,128]{2,1,0:T(8,128)(2,1)S(1)}, u32[]{:S(2)}, u32[]{:S(2)}) collective-permute-start(bf16[1,256,128]{2,1,0:T(8,128)(2,1)S(1)} %get-tuple-element.32), channel_id=1, source_target_pairs={{0,8},{8,16},{16,24},{24,32},{32,40},{40,48},{48,56},{56,64},{64,7... | collective-permute-start | bytes 196616 | tf_op jit(solution)/shard_map/ppermute | solution.py:17
  19.0 5.2 %collective-permute-start.1 = (bf16[1,256,128]{2,1,0:T(8,128)(2,1)S(1)}, bf16[1,256,128]{2,1,0:T(8,128)(2,1)S(1)}, u32[]{:S(2)}, u32[]{:S(2)}) collective-permute-start(bf16[1,256,128]{2,1,0:T(8,128)(2,1)S(1)} %get-tuple-element.33), channel_id=1, source_target_pairs={{8,0},{16,8},{24,16},{32,24},{40,32},{48,40},{56,48},{64,56},{72,6... | collective-permute-start | bytes 196616 | tf_op jit(solution)/shard_map/ppermute | solution.py:18
  25.0 124.2 %all-gather.5.cloned.1.call-start = ((), (), s32[]{:S(2)}) async-start(), calls=%async_computation.5 | async-start | bytes 3538944 | tf_op jit(solution)/shard_map/all_gather | solution.py:100
  76.3 1.8 copy-start.5
  78.1 1.9 copy-start.3
  78.1 3.7 %copy-start.7 = (bf16[3,3,1024,128]{3,2,1,0:T(8,128)(2,1)S(1)}, bf16[3,3,1024,128]{3,2,1,0:T(8,128)(2,1)}, u32[]{:S(2)}) copy-start(bf16[3,3,1024,128]{3,2,1,0:T(8,128)(2,1)} %param.17) | copy-start | bytes 7077892
  79.9 1.8 copy-start.1
  85.5 19.8 %copy-start.12 = (f32[128]{0:T(128)S(1)}, f32[128]{0:T(128)}, u32[]{:S(2)}) copy-start(f32[128]{0:T(128)} %param.19) | copy-start | bytes 1540
  85.5 19.8 %copy-start.13 = (f32[128]{0:T(128)S(1)}, f32[128]{0:T(128)}, u32[]{:S(2)}) copy-start(f32[128]{0:T(128)} %param.18) | copy-start | bytes 1540
  105.5 3.7 %collective-permute-start.2 = (bf16[1,256,128]{2,1,0:T(8,128)(2,1)S(1)}, bf16[1,256,128]{2,1,0:T(8,128)(2,1)S(1)}, u32[]{:S(2)}, u32[]{:S(2)}) collective-permute-start(bf16[1,256,128]{2,1,0:T(8,128)(2,1)S(1)} %get-tuple-element.30), channel_id=1, source_target_pairs={{0,8},{8,16},{16,24},{24,32},{32,40},{40,48},{48,56},{56,64},{64,7... | collective-permute-start | bytes 196616 | tf_op jit(solution)/shard_map/ppermute | solution.py:17
  107.7 5.0 %collective-permute-start.3 = (bf16[1,256,128]{2,1,0:T(8,128)(2,1)S(1)}, bf16[1,256,128]{2,1,0:T(8,128)(2,1)S(1)}, u32[]{:S(2)}, u32[]{:S(2)}) collective-permute-start(bf16[1,256,128]{2,1,0:T(8,128)(2,1)S(1)} %get-tuple-element.31), channel_id=1, source_target_pairs={{8,0},{16,8},{24,16},{32,24},{40,32},{48,40},{56,48},{64,56},{72,6... | collective-permute-start | bytes 196616 | tf_op jit(solution)/shard_map/ppermute | solution.py:18
  162.2 1.8 copy-start.6
  164.0 1.9 copy-start.4
  164.0 3.7 %copy-start.8 = (bf16[3,3,1024,128]{3,2,1,0:T(8,128)(2,1)S(1)}, bf16[3,3,1024,128]{3,2,1,0:T(8,128)(2,1)}, u32[]{:S(2)}) copy-start(bf16[3,3,1024,128]{3,2,1,0:T(8,128)(2,1)} %param.20) | copy-start | bytes 7077892
  165.9 1.8 copy-start.2
  171.4 19.8 %copy-start.14 = (f32[128]{0:T(128)S(1)}, f32[128]{0:T(128)}, u32[]{:S(2)}) copy-start(f32[128]{0:T(128)} %param.22) | copy-start | bytes 1540
  171.4 19.8 %copy-start.15 = (f32[128]{0:T(128)S(1)}, f32[128]{0:T(128)}, u32[]{:S(2)}) copy-start(f32[128]{0:T(128)} %param.21) | copy-start | bytes 1540
  191.5 1.8 copy-start.9
  193.3 6.0 %copy-start.10 = (s32[4,256]{1,0:T(4,128)S(1)}, s32[4,256]{1,0:T(4,128)}, u32[]{:S(2)}) copy-start(s32[4,256]{1,0:T(4,128)} %param.12) | copy-start | bytes 12292
  193.3 32.4 %all-to-all-start.2 = ((bf16[8,4,256,128]{3,2,1,0:T(8,128)(2,1)}), bf16[8,4,256,128]{3,2,1,0:T(8,128)(2,1)}, u32[]{:S(2)}, u32[]{:S(2)}) async-start(bf16[8,4,256,128]{3,2,1,0:T(8,128)(2,1)} %broadcast_in_dim.62), calls=%async_computation.2 | async-start | bytes 4194304 | tf_op jit(solution)/shard_map/all_to_all | solution.py:25
  233.2 9.5 %all-to-all-start.3 = ((f32[8,3,1024]{2,1,0:T(4,128)}), f32[8,3,1024]{2,1,0:T(4,128)S(1)}, u32[]{:S(2)}, u32[]{:S(2)}) async-start(f32[8,3,1024]{2,1,0:T(4,128)} %broadcast_in_dim.64), calls=%async_computation.3 | async-start | bytes 262144 | tf_op jit(solution)/shard_map/all_to_all | solution.py:25
Sparse Core Ops, SparseCore 0:
  25.1 38.1 all-gather.2
  113.7 35.5 all-gather.4
where the time goes:
time: 251 us
  waiting for transfers between devices  113 us (45%)
  local copies, waits for them, and re-layouts  38.3 us (15%)
  blocking collectives  36.1 us (14%)
  matrix products  22.1 us (9%)
  starting transfers between devices  19.7 us (8%)
  between operations  14.6 us (6%)
  other arithmetic  7.12 us (3%)
    all_gather x2, waiting for transfers between devices, convolve(): lax.all_gather(rimmed, 'cols', axis=2, tiled=True)  73.9 us
    all_to_all x2, blocking collectives, sent_to_all(): return lax.all_to_all(copies, axis, split_axis=0, concat_axis=0, tiled=True)  36.1 us
    all_to_all x2, waiting for transfers between devices, sent_to_all(): return lax.all_to_all(copies, axis, split_axis=0, concat_axis=0, tiled=True)  31.6 us
    slice x2, local copies, waits for them, and re-layouts, add_taps(): padded[shift_row:shift_row + rows_here, shift_col:shift_col + width]  26 us
    dot_general x18, matrix products, add_taps(): total = total + jnp.dot(window, taps, preferred_element_type=jnp.float32)  19.7 us
    all_to_all x2, starting transfers between devices, sent_to_all(): return lax.all_to_all(copies, axis, split_axis=0, concat_axis=0, tiled=True)  10.3 us
    ppermute x2, waiting for transfers between devices, with_halo(): after = lax.ppermute(leading, axis, down)  7.4 us
    ppermute x2, starting transfers between devices, with_halo(): before = lax.ppermute(last, axis, up)  6.61 us
  transfers between devices with their start and end apart: 8, of which 6 were waited for; matrix products, arithmetic and copies ran while one was open for 0% of the time, Pallas kernels for 0%

commit v1 on v0

--- a/solution.py
+++ b/solution.py
@@ -5,6 +5,24 @@
 
 C = 1024
 GROUPS = 32
+
+
+def ring_gather(shard, axis, dim):
+    ways, here, turn = (lax.axis_size(axis), lax.axis_index(axis), shard.shape[dim])
+    shape = [n * ways if d == dim else n for d, n in enumerate(shard.shape)]
+    full = lax.dynamic_update_slice_in_dim(
+        jnp.zeros(shape, shard.dtype), shard, here * turn, axis=dim
+    )
+    going_up = going_down = shard
+    for far in range(1, ways // 2 + 1):
+        going_up = lax.ppermute(going_up, axis, [(d, (d + 1) % ways) for d in range(ways)])
+        full = lax.dynamic_update_slice_in_dim(full, going_up, (here - far) % ways * turn, axis=dim)
+        if 2 * far < ways:
+            going_down = lax.ppermute(going_down, axis, [(d, (d - 1) % ways) for d in range(ways)])
+            full = lax.dynamic_update_slice_in_dim(
+                full, going_down, (here + far) % ways * turn, axis=dim
+            )
+    return full
 
 
 def with_halo(value, sides, width):
@@ -97,7 +115,7 @@
     rows_here, width, _ = field.shape
     empty = jnp.zeros((rows_here * width, weight.shape[3]), jnp.float32)
     rimmed = with_halo(field, (("rows", 0),), 1)
-    total = add_taps(empty, weight, lax.all_gather(rimmed, "cols", axis=2, tiled=True))
+    total = add_taps(empty, weight, ring_gather(rimmed, "cols", 2))
     return total.reshape(rows_here, width, -1)
 
 

time: 251 us -> 232 us (0.924)
  waiting for transfers between devices: 113 us -> 57.9 us
  starting transfers between devices: 19.7 us -> 63.1 us
  between operations: 14.6 us -> 1.19 us
  local copies, waits for them, and re-layouts: 38.3 us -> 46 us
    all_gather x2 -> x0, waiting for transfers between devices: 73.9 us -> none  [convolve(): lax.all_gather(rimmed, 'cols', axis=2, tiled=True)]
    ppermute x0 -> x14, starting transfers between devices: none -> 34.8 us  [the longest x8 18.3 us: ring_gather(): lax.ppermute(going_up, axis, [(d, (d + 1) % ways) for d in range(ways)])]
    ppermute x0 -> x14, waiting for transfers between devices: none -> 21.3 us  [the longest x8 21.2 us: ring_gather(): lax.ppermute(going_up, axis, [(d, (d + 1) % ways) for d in range(ways)])]
    dynamic_update_slice x0 -> x14, local copies, waits for them, and re-layouts: none -> 9.69 us  [the longest x8 5.85 us: ring_gather(): lax.dynamic_update_slice_in_dim(full, going_up, (here - far) % ways * tur...]
    all_to_all x2, starting transfers between devices: 10.3 us -> 17.2 us  [sent_to_all(): return lax.all_to_all(copies, axis, split_axis=0, concat_axis=0, tiled=True)]
    slice x2, local copies, waits for them, and re-layouts: 26 us -> 21.3 us  [add_taps(): padded[shift_row:shift_row + rows_here, shift_col:shift_col + width]]
    ppermute x2, waiting for transfers between devices: 7.4 us -> 3.88 us  [with_halo(): after = lax.ppermute(leading, axis, down)]
  transfers between devices with their start and end apart: 8 -> 20, of which waited for: 6 -> 12; matrix products, arithmetic and copies ran while one was open for 0% -> 4% of each run, Pallas kernels for 0% -> 0%
where the time goes in v1:
time: 232 us; the launch traced here: 231 us
  starting transfers between devices  63.1 us (27%)
  waiting for transfers between devices  57.9 us (25%)
  local copies, waits for them, and re-layouts  46 us (20%)
  blocking collectives  35 us (15%)
  matrix products  21.3 us (9%)
  other arithmetic  6.73 us (3%)
    all_to_all x2, blocking collectives, sent_to_all(): return lax.all_to_all(copies, axis, split_axis=0, concat_axis=0, tiled=True)  35 us
    all_to_all x2, waiting for transfers between devices, sent_to_all(): return lax.all_to_all(copies, axis, split_axis=0, concat_axis=0, tiled=True)  31.6 us
    slice x2, local copies, waits for them, and re-layouts, add_taps(): padded[shift_row:shift_row + rows_here, shift_col:shift_col + width]  21.3 us
    ppermute x8, waiting for transfers between devices, ring_gather(): lax.ppermute(going_up, axis, [(d, (d + 1) % ways) for d in range(ways)])  21.2 us
    dot_general x18, matrix products, add_taps(): total = total + jnp.dot(window, taps, preferred_element_type=jnp.float32)  18.9 us
    ppermute x8, starting transfers between devices, ring_gather(): lax.ppermute(going_up, axis, [(d, (d + 1) % ways) for d in range(ways)])  18.3 us
    all_to_all x2, starting transfers between devices, sent_to_all(): return lax.all_to_all(copies, axis, split_axis=0, concat_axis=0, tiled=True)  17.2 us
    ppermute x6, starting transfers between devices, ring_gather(): lax.ppermute(going_down, axis, [(d, (d - 1) % ways) for d in range(ways)])  16.5 us
  transfers between devices with their start and end apart: 20, of which 12 were waited for; matrix products, arithmetic and copies ran while one was open for 4% of the time, Pallas kernels for 0%

profile of v1, /device:TPU:1, one launch (start us, length us, event | category | flops | bytes accessed | tf_op | source)
XLA Modules:
  0.0 231.2 jit_solution(9607987156133763611)
XLA Ops:
  2.9 4.7 %gather_fusion = bf16[1024,128]{1,0:T(8,128)(2,1)S(1)} fusion(bf16[8192,128]{1,0:T(8,128)(2,1)} %param.15, s32[1024]{0:T(1024)S(1)} %broadcast_clamp_fusion), kind=kCustom, calls=%fused_computation | custom fusion | bytes 528384 | tf_op jit(solution)/shard_map/jit(_take)/gather | solution.py:162
  8.1 4.4 %collective-permute-start = (bf16[1,256,128]{2,1,0:T(8,128)(2,1)S(1)}, bf16[1,256,128]{2,1,0:T(8,128)(2,1)S(1)}, u32[]{:S(2)}, u32[]{:S(2)}) collective-permute-start(bf16[1,256,128]{2,1,0:T(8,128)(2,1)S(1)} %get-tuple-element.36), channel_id=1, source_target_pairs={{0,8},{8,16},{16,24},{24,32},{32,40},{40,48},{48,56},{56,64},{64,7... | collective-permute-start | bytes 196616 | tf_op jit(solution)/shard_map/ppermute | solution.py:35
  13.7 3.9 %collective-permute-done.1 = bf16[1,256,128]{2,1,0:T(8,128)(2,1)S(1)} collective-permute-done((bf16[1,256,128]{2,1,0:T(8,128)(2,1)S(1)}, bf16[1,256,128]{2,1,0:T(8,128)(2,1)S(1)}, u32[]{:S(2)}, u32[]{:S(2)}) %collective-permute-start.1) | collective-permute-done | bytes 65568 | tf_op jit(solution)/shard_map/ppermute | solution.py:36
  20.6 3.0 %collective-permute-start.2 = (bf16[6,256,128]{2,1,0:T(8,128)(2,1)S(1)}, bf16[6,256,128]{2,1,0:T(8,128)(2,1)S(1)}, u32[]{:S(2)}, u32[]{:S(2)}) collective-permute-start(bf16[6,256,128]{2,1,0:T(8,128)(2,1)S(1)} %get-tuple-element.32), channel_id=1, source_target_pairs={{0,1},{1,2},{2,3},{3,4},{4,5},{5,6},{6,7},{7,0},{8,9},{9,10},{10,1... | collective-permute-start | bytes 1179656 | tf_op jit(solution)/shard_map/ppermute | solution.py:18
  23.6 4.7 %collective-permute-done.2 = bf16[6,256,128]{2,1,0:T(8,128)(2,1)S(1)} collective-permute-done((bf16[6,256,128]{2,1,0:T(8,128)(2,1)S(1)}, bf16[6,256,128]{2,1,0:T(8,128)(2,1)S(1)}, u32[]{:S(2)}, u32[]{:S(2)}) %collective-permute-start.2) | collective-permute-done | bytes 393248 | tf_op jit(solution)/shard_map/ppermute | solution.py:18
  28.3 2.5 %collective-permute-start.4 = (bf16[6,256,128]{2,1,0:T(8,128)(2,1)S(1)}, bf16[6,256,128]{2,1,0:T(8,128)(2,1)S(1)}, u32[]{:S(2)}, u32[]{:S(2)}) collective-permute-start(bf16[6,256,128]{2,1,0:T(8,128)(2,1)S(1)} %collective-permute-done.2), channel_id=1, source_target_pairs={{0,1},{1,2},{2,3},{3,4},{4,5},{5,6},{6,7},{7,0},{8,9},{9,10},{10,1... | collective-permute-start | bytes 1179656 | tf_op jit(solution)/shard_map/ppermute | solution.py:18
  31.0 4.6 %collective-permute-done.4 = bf16[6,256,128]{2,1,0:T(8,128)(2,1)S(1)} collective-permute-done((bf16[6,256,128]{2,1,0:T(8,128)(2,1)S(1)}, bf16[6,256,128]{2,1,0:T(8,128)(2,1)S(1)}, u32[]{:S(2)}, u32[]{:S(2)}) %collective-permute-start.4) | collective-permute-done | bytes 393248 | tf_op jit(solution)/shard_map/ppermute | solution.py:18
  35.5 2.5 %collective-permute-start.6 = (bf16[6,256,128]{2,1,0:T(8,128)(2,1)S(1)}, bf16[6,256,128]{2,1,0:T(8,128)(2,1)}, u32[]{:S(2)}, u32[]{:S(2)}) collective-permute-start(bf16[6,256,128]{2,1,0:T(8,128)(2,1)S(1)} %collective-permute-done.4), channel_id=1, source_target_pairs={{0,1},{1,2},{2,3},{3,4},{4,5},{5,6},{6,7},{7,0},{8,9},{9,10},{10,1... | collective-permute-start | bytes 1179656 | tf_op jit(solution)/shard_map/ppermute | solution.py:18
  51.2 12.9 %pad_slice_fusion.11 = (bf16[4,256,1024]{2,1,0:T(8,128)(2,1)}, bf16[4,256,1024]{2,1,0:T(8,128)(2,1)S(1)}, bf16[4,256,1024]{2,1,0:T(8,128)(2,1)S(1)}, bf16[4,256,...) fusion(bf16[6,256,1024]{2,1,0:T(8,128)(2,1)} %constant_dynamic-, ...), kind=kLoop, calls=%fused_computation.17 | loop fusion | bytes 28311552 | tf_op jit(solution)/shard_map/slice | solution.py:106
  64.1 2.4 %fusion.34 = f32[1024,128]{1,0:T(8,128)S(1)} fusion(bf16[1024,1024]{1,0:T(8,128)(2,1)} %bitcast.137, bf16[3,3,1024,128]{3,2,1,0:T(8,128)(2,1)} %param.17), kind=kOutput, calls=%fused_computation.57 | convolution fusion | flops 268435456 | bytes 2883584 | tf_op jit(solution)/shard_map/dot_general | solution.py:110
  74.0 19.5 %all_to_all.22 = f32[32,1,8]{2,1,0:T(1,128)S(1)} all-to-all(f32[32,1,8]{2,1,0:T(1,128)S(1)} %broadcast_in_dim.60), channel_id=1, replica_groups=mesh['rows'=32,'cols'=8] {'rows'}, dimensions={0} | all-to-all | bytes 2048 | tf_op jit(solution)/shard_map/all_to_all | solution.py:43
  95.5 4.2 %collective-permute-start.9 = (bf16[1,256,128]{2,1,0:T(8,128)(2,1)S(1)}, bf16[1,256,128]{2,1,0:T(8,128)(2,1)S(1)}, u32[]{:S(2)}, u32[]{:S(2)}) collective-permute-start(bf16[1,256,128]{2,1,0:T(8,128)(2,1)S(1)} %get-tuple-element.34), channel_id=1, source_target_pairs={{0,8},{8,16},{16,24},{24,32},{32,40},{40,48},{48,56},{56,64},{64,7... | collective-permute-start | bytes 196616 | tf_op jit(solution)/shard_map/ppermute | solution.py:35
  101.5 4.9 %collective-permute-start.11 = (bf16[6,256,128]{2,1,0:T(8,128)(2,1)S(1)}, bf16[6,256,128]{2,1,0:T(8,128)(2,1)S(1)}, u32[]{:S(2)}, u32[]{:S(2)}) collective-permute-start(bf16[6,256,128]{2,1,0:T(8,128)(2,1)S(1)} %get-tuple-element.30), channel_id=1, source_target_pairs={{0,1},{1,2},{2,3},{3,4},{4,5},{5,6},{6,7},{7,0},{8,9},{9,10},{10,1... | collective-permute-start | bytes 1179656 | tf_op jit(solution)/shard_map/ppermute | solution.py:18
  106.4 3.8 %collective-permute-start.12 = (bf16[6,256,128]{2,1,0:T(8,128)(2,1)S(1)}, bf16[6,256,128]{2,1,0:T(8,128)(2,1)S(1)}, u32[]{:S(2)}, u32[]{:S(2)}) collective-permute-start(bf16[6,256,128]{2,1,0:T(8,128)(2,1)S(1)} %get-tuple-element.30), channel_id=1, source_target_pairs={{0,7},{1,0},{2,1},{3,2},{4,3},{5,4},{6,5},{7,6},{8,15},{9,8},{10,9... | collective-permute-start | bytes 1179656 | tf_op jit(solution)/shard_map/ppermute | solution.py:21
  113.6 5.0 %collective-permute-start.14 = (bf16[6,256,128]{2,1,0:T(8,128)(2,1)S(1)}, bf16[6,256,128]{2,1,0:T(8,128)(2,1)S(1)}, u32[]{:S(2)}, u32[]{:S(2)}) collective-permute-start(bf16[6,256,128]{2,1,0:T(8,128)(2,1)S(1)} %collective-permute-done.12), channel_id=1, source_target_pairs={{0,7},{1,0},{2,1},{3,2},{4,3},{5,4},{6,5},{7,6},{8,15},{9,8},{10,9... | collective-permute-start | bytes 1179656 | tf_op jit(solution)/shard_map/ppermute | solution.py:21
  120.9 6.2 %collective-permute-start.16 = (bf16[6,256,128]{2,1,0:T(8,128)(2,1)S(1)}, bf16[6,256,128]{2,1,0:T(8,128)(2,1)S(1)}, u32[]{:S(2)}, u32[]{:S(2)}) collective-permute-start(bf16[6,256,128]{2,1,0:T(8,128)(2,1)S(1)} %collective-permute-done.14), channel_id=1, source_target_pairs={{0,7},{1,0},{2,1},{3,2},{4,3},{5,4},{6,5},{7,6},{8,15},{9,8},{10,9... | collective-permute-start | bytes 1179656 | tf_op jit(solution)/shard_map/ppermute | solution.py:21
  128.8 7.8 %collective-permute-done.17 = bf16[6,256,128]{2,1,0:T(8,128)(2,1)S(1)} collective-permute-done((bf16[6,256,128]{2,1,0:T(8,128)(2,1)S(1)}, bf16[6,256,128]{2,1,0:T(8,128)(2,1)S(1)}, u32[]{:S(2)}, u32[]{:S(2)}) %collective-permute-start.17) | collective-permute-done | bytes 393248 | tf_op jit(solution)/shard_map/ppermute | solution.py:18
  136.8 8.4 %pad_slice_fusion.5 = (bf16[4,256,1024]{2,1,0:T(8,128)(2,1)}, bf16[4,256,1024]{2,1,0:T(8,128)(2,1)S(1)}, bf16[4,256,1024]{2,1,0:T(8,128)(2,1)S(1)}, bf16[4,256,1...) fusion(bf16[6,256,1024]{2,1,0:T(8,128)(2,1)S(1)} %constant_dyna, ...), kind=kLoop, calls=%fused_computation.11 | loop fusion | bytes 28311552 | tf_op jit(solution)/shard_map/slice | solution.py:106
  155.6 15.5 %all_to_all.23 = f32[32,1,8]{2,1,0:T(1,128)S(1)} all-to-all(f32[32,1,8]{2,1,0:T(1,128)S(1)} %broadcast_in_dim.61), channel_id=1, replica_groups=mesh['rows'=32,'cols'=8] {'rows'}, dimensions={0} | all-to-all | bytes 2048 | tf_op jit(solution)/shard_map/all_to_all | solution.py:43
  173.7 13.0 %all-to-all-start.2 = ((bf16[8,4,256,128]{3,2,1,0:T(8,128)(2,1)}), bf16[8,4,256,128]{3,2,1,0:T(8,128)(2,1)}, u32[]{:S(2)}, u32[]{:S(2)}) async-start(bf16[8,4,256,128]{3,2,1,0:T(8,128)(2,1)} %broadcast_in_dim.62), calls=%async_computation.2 | async-start | bytes 4194304 | tf_op jit(solution)/shard_map/all_to_all | solution.py:43
  186.7 26.3 %all-to-all-done.2 = bf16[8,4,256,128]{3,2,1,0:T(8,128)(2,1)} async-done(((bf16[8,4,256,128]{3,2,1,0:T(8,128)(2,1)}), bf16[8,4,256,128]{3,2,1,0:T(8,128)(2,1)}, u32[]{:S(2)}, u32[]{:S(2)}) %all-to-all-start.2) | async-done | bytes 2097184 | tf_op jit(solution)/shard_map/all_to_all | solution.py:43
  213.0 2.9 %copy.22 = bf16[4,256,8,128]{3,2,1,0:T(8,128)(2,1)S(1)} copy(bf16[4,256,8,128]{3,1,0,2:T(8,128)(2,1)} %bitcast.39) | data formatting | bytes 4194304 | tf_op jit(solution)/shard_map/transpose | solution.py:59
  220.5 4.2 %all-to-all-start.3 = ((f32[8,3,1024]{2,1,0:T(4,128)}), f32[8,3,1024]{2,1,0:T(4,128)S(1)}, u32[]{:S(2)}, u32[]{:S(2)}) async-start(f32[8,3,1024]{2,1,0:T(4,128)} %broadcast_in_dim.64), calls=%async_computation.3 | async-start | bytes 262144 | tf_op jit(solution)/shard_map/all_to_all | solution.py:43
  224.7 5.3 %all-to-all-done.3 = f32[8,3,1024]{2,1,0:T(4,128)S(1)} async-done(((f32[8,3,1024]{2,1,0:T(4,128)}), f32[8,3,1024]{2,1,0:T(4,128)S(1)}, u32[]{:S(2)}, u32[]{:S(2)}) %all-to-all-start.3) | async-done | bytes 98336 | tf_op jit(solution)/shard_map/all_to_all | solution.py:43
  (157 shorter events, 57.4 us)
Async XLA Ops:
  0.6 215.3 %copy-start = (bf16[1024,1024]{1,0:T(8,128)(2,1)S(1)}, bf16[1024,1024]{1,0:T(8,128)(2,1)}, u32[]{:S(2)}) copy-start(bf16[1024,1024]{1,0:T(8,128)(2,1)} %param.23) | copy-start | bytes 6291460
  8.1 5.7 %collective-permute-start = (bf16[1,256,128]{2,1,0:T(8,128)(2,1)S(1)}, bf16[1,256,128]{2,1,0:T(8,128)(2,1)S(1)}, u32[]{:S(2)}, u32[]{:S(2)}) collective-permute-start(bf16[1,256,128]{2,1,0:T(8,128)(2,1)S(1)} %get-tuple-element.36), channel_id=1, source_target_pairs={{0,8},{8,16},{16,24},{24,32},{32,40},{40,48},{48,56},{56,64},{64,7... | collective-permute-start | bytes 196616 | tf_op jit(solution)/shard_map/ppermute | solution.py:35
  12.4 5.2 %collective-permute-start.1 = (bf16[1,256,128]{2,1,0:T(8,128)(2,1)S(1)}, bf16[1,256,128]{2,1,0:T(8,128)(2,1)S(1)}, u32[]{:S(2)}, u32[]{:S(2)}) collective-permute-start(bf16[1,256,128]{2,1,0:T(8,128)(2,1)S(1)} %get-tuple-element.37), channel_id=1, source_target_pairs={{8,0},{16,8},{24,16},{32,24},{40,32},{48,40},{56,48},{64,56},{72,6... | collective-permute-start | bytes 196616 | tf_op jit(solution)/shard_map/ppermute | solution.py:36
  20.6 7.7 %collective-permute-start.2 = (bf16[6,256,128]{2,1,0:T(8,128)(2,1)S(1)}, bf16[6,256,128]{2,1,0:T(8,128)(2,1)S(1)}, u32[]{:S(2)}, u32[]{:S(2)}) collective-permute-start(bf16[6,256,128]{2,1,0:T(8,128)(2,1)S(1)} %get-tuple-element.32), channel_id=1, source_target_pairs={{0,1},{1,2},{2,3},{3,4},{4,5},{5,6},{6,7},{7,0},{8,9},{9,10},{10,1... | collective-permute-start | bytes 1179656 | tf_op jit(solution)/shard_map/ppermute | solution.py:18
  23.6 7.3 %collective-permute-start.3 = (bf16[6,256,128]{2,1,0:T(8,128)(2,1)S(1)}, bf16[6,256,128]{2,1,0:T(8,128)(2,1)}, u32[]{:S(2)}, u32[]{:S(2)}) collective-permute-start(bf16[6,256,128]{2,1,0:T(8,128)(2,1)S(1)} %get-tuple-element.32), channel_id=1, source_target_pairs={{0,7},{1,0},{2,1},{3,2},{4,3},{5,4},{6,5},{7,6},{8,15},{9,8},{10,9... | collective-permute-start | bytes 1179656 | tf_op jit(solution)/shard_map/ppermute | solution.py:21
  28.3 7.2 %collective-permute-start.4 = (bf16[6,256,128]{2,1,0:T(8,128)(2,1)S(1)}, bf16[6,256,128]{2,1,0:T(8,128)(2,1)S(1)}, u32[]{:S(2)}, u32[]{:S(2)}) collective-permute-start(bf16[6,256,128]{2,1,0:T(8,128)(2,1)S(1)} %collective-permute-done.2), channel_id=1, source_target_pairs={{0,1},{1,2},{2,3},{3,4},{4,5},{5,6},{6,7},{7,0},{8,9},{9,10},{10,1... | collective-permute-start | bytes 1179656 | tf_op jit(solution)/shard_map/ppermute | solution.py:18
  30.9 8.9 %collective-permute-start.5 = (bf16[6,256,128]{2,1,0:T(8,128)(2,1)}, bf16[6,256,128]{2,1,0:T(8,128)(2,1)S(1)}, u32[]{:S(2)}, u32[]{:S(2)}) collective-permute-start(bf16[6,256,128]{2,1,0:T(8,128)(2,1)} %collective-permute-done.3), channel_id=1, source_target_pairs={{0,7},{1,0},{2,1},{3,2},{4,3},{5,4},{6,5},{7,6},{8,15},{9,8},{10,9... | collective-permute-start | bytes 1179656 | tf_op jit(solution)/shard_map/ppermute | solution.py:21
  35.5 7.5 %collective-permute-start.6 = (bf16[6,256,128]{2,1,0:T(8,128)(2,1)S(1)}, bf16[6,256,128]{2,1,0:T(8,128)(2,1)}, u32[]{:S(2)}, u32[]{:S(2)}) collective-permute-start(bf16[6,256,128]{2,1,0:T(8,128)(2,1)S(1)} %collective-permute-done.4), channel_id=1, source_target_pairs={{0,1},{1,2},{2,3},{3,4},{4,5},{5,6},{6,7},{7,0},{8,9},{9,10},{10,1... | collective-permute-start | bytes 1179656 | tf_op jit(solution)/shard_map/ppermute | solution.py:18
  39.8 8.9 %collective-permute-start.7 = (bf16[6,256,128]{2,1,0:T(8,128)(2,1)S(1)}, bf16[6,256,128]{2,1,0:T(8,128)(2,1)S(1)}, u32[]{:S(2)}, u32[]{:S(2)}) collective-permute-start(bf16[6,256,128]{2,1,0:T(8,128)(2,1)S(1)} %collective-permute-done.5), channel_id=1, source_target_pairs={{0,7},{1,0},{2,1},{3,2},{4,3},{5,4},{6,5},{7,6},{8,15},{9,8},{10,9... | collective-permute-start | bytes 1179656 | tf_op jit(solution)/shard_map/ppermute | solution.py:21
  43.0 7.3 %collective-permute-start.8 = (bf16[6,256,128]{2,1,0:T(8,128)(2,1)}, bf16[6,256,128]{2,1,0:T(8,128)(2,1)S(1)}, u32[]{:S(2)}, u32[]{:S(2)}) collective-permute-start(bf16[6,256,128]{2,1,0:T(8,128)(2,1)} %collective-permute-done.6), channel_id=1, source_target_pairs={{0,1},{1,2},{2,3},{3,4},{4,5},{5,6},{6,7},{7,0},{8,9},{9,10},{10,1... | collective-permute-start | bytes 1179656 | tf_op jit(solution)/shard_map/ppermute | solution.py:18
  72.7 21.4 %copy-start.13 = (f32[128]{0:T(128)S(1)}, f32[128]{0:T(128)}, u32[]{:S(2)}) copy-start(f32[128]{0:T(128)} %param.19) | copy-start | bytes 1540
  72.7 21.4 %copy-start.14 = (f32[128]{0:T(128)S(1)}, f32[128]{0:T(128)}, u32[]{:S(2)}) copy-start(f32[128]{0:T(128)} %param.18) | copy-start | bytes 1540
  94.2 5.5 %collective-permute-start.10 = (bf16[1,256,128]{2,1,0:T(8,128)(2,1)S(1)}, bf16[1,256,128]{2,1,0:T(8,128)(2,1)S(1)}, u32[]{:S(2)}, u32[]{:S(2)}) collective-permute-start(bf16[1,256,128]{2,1,0:T(8,128)(2,1)S(1)} %get-tuple-element.35), channel_id=1, source_target_pairs={{8,0},{16,8},{24,16},{32,24},{40,32},{48,40},{56,48},{64,56},{72,6... | collective-permute-start | bytes 196616 | tf_op jit(solution)/shard_map/ppermute | solution.py:36
  95.5 5.3 %collective-permute-start.9 = (bf16[1,256,128]{2,1,0:T(8,128)(2,1)S(1)}, bf16[1,256,128]{2,1,0:T(8,128)(2,1)S(1)}, u32[]{:S(2)}, u32[]{:S(2)}) collective-permute-start(bf16[1,256,128]{2,1,0:T(8,128)(2,1)S(1)} %get-tuple-element.34), channel_id=1, source_target_pairs={{0,8},{8,16},{16,24},{24,32},{32,40},{40,48},{48,56},{56,64},{64,7... | collective-permute-start | bytes 196616 | tf_op jit(solution)/shard_map/ppermute | solution.py:35
  101.5 9.9 %collective-permute-start.11 = (bf16[6,256,128]{2,1,0:T(8,128)(2,1)S(1)}, bf16[6,256,128]{2,1,0:T(8,128)(2,1)S(1)}, u32[]{:S(2)}, u32[]{:S(2)}) collective-permute-start(bf16[6,256,128]{2,1,0:T(8,128)(2,1)S(1)} %get-tuple-element.30), channel_id=1, source_target_pairs={{0,1},{1,2},{2,3},{3,4},{4,5},{5,6},{6,7},{7,0},{8,9},{9,10},{10,1... | collective-permute-start | bytes 1179656 | tf_op jit(solution)/shard_map/ppermute | solution.py:18
  106.4 7.2 %collective-permute-start.12 = (bf16[6,256,128]{2,1,0:T(8,128)(2,1)S(1)}, bf16[6,256,128]{2,1,0:T(8,128)(2,1)S(1)}, u32[]{:S(2)}, u32[]{:S(2)}) collective-permute-start(bf16[6,256,128]{2,1,0:T(8,128)(2,1)S(1)} %get-tuple-element.30), channel_id=1, source_target_pairs={{0,7},{1,0},{2,1},{3,2},{4,3},{5,4},{6,5},{7,6},{8,15},{9,8},{10,9... | collective-permute-start | bytes 1179656 | tf_op jit(solution)/shard_map/ppermute | solution.py:21
  111.4 8.4 %collective-permute-start.13 = (bf16[6,256,128]{2,1,0:T(8,128)(2,1)S(1)}, bf16[6,256,128]{2,1,0:T(8,128)(2,1)S(1)}, u32[]{:S(2)}, u32[]{:S(2)}) collective-permute-start(bf16[6,256,128]{2,1,0:T(8,128)(2,1)S(1)} %collective-permute-done.11), channel_id=1, source_target_pairs={{0,1},{1,2},{2,3},{3,4},{4,5},{5,6},{6,7},{7,0},{8,9},{9,10},{10,1... | collective-permute-start | bytes 1179656 | tf_op jit(solution)/shard_map/ppermute | solution.py:18
  113.6 7.3 %collective-permute-start.14 = (bf16[6,256,128]{2,1,0:T(8,128)(2,1)S(1)}, bf16[6,256,128]{2,1,0:T(8,128)(2,1)S(1)}, u32[]{:S(2)}, u32[]{:S(2)}) collective-permute-start(bf16[6,256,128]{2,1,0:T(8,128)(2,1)S(1)} %collective-permute-done.12), channel_id=1, source_target_pairs={{0,7},{1,0},{2,1},{3,2},{4,3},{5,4},{6,5},{7,6},{8,15},{9,8},{10,9... | collective-permute-start | bytes 1179656 | tf_op jit(solution)/shard_map/ppermute | solution.py:21
  119.8 8.4 %collective-permute-start.15 = (bf16[6,256,128]{2,1,0:T(8,128)(2,1)S(1)}, bf16[6,256,128]{2,1,0:T(8,128)(2,1)S(1)}, u32[]{:S(2)}, u32[]{:S(2)}) collective-permute-start(bf16[6,256,128]{2,1,0:T(8,128)(2,1)S(1)} %collective-permute-done.13), channel_id=1, source_target_pairs={{0,1},{1,2},{2,3},{3,4},{4,5},{5,6},{6,7},{7,0},{8,9},{9,10},{10,1... | collective-permute-start | bytes 1179656 | tf_op jit(solution)/shard_map/ppermute | solution.py:18
  120.9 7.7 %collective-permute-start.16 = (bf16[6,256,128]{2,1,0:T(8,128)(2,1)S(1)}, bf16[6,256,128]{2,1,0:T(8,128)(2,1)S(1)}, u32[]{:S(2)}, u32[]{:S(2)}) collective-permute-start(bf16[6,256,128]{2,1,0:T(8,128)(2,1)S(1)} %collective-permute-done.14), channel_id=1, source_target_pairs={{0,7},{1,0},{2,1},{3,2},{4,3},{5,4},{6,5},{7,6},{8,15},{9,8},{10,9... | collective-permute-start | bytes 1179656 | tf_op jit(solution)/shard_map/ppermute | solution.py:21
  128.2 8.4 %collective-permute-start.17 = (bf16[6,256,128]{2,1,0:T(8,128)(2,1)S(1)}, bf16[6,256,128]{2,1,0:T(8,128)(2,1)S(1)}, u32[]{:S(2)}, u32[]{:S(2)}) collective-permute-start(bf16[6,256,128]{2,1,0:T(8,128)(2,1)S(1)} %collective-permute-done.15), channel_id=1, source_target_pairs={{0,1},{1,2},{2,3},{3,4},{4,5},{5,6},{6,7},{7,0},{8,9},{9,10},{10,1... | collective-permute-start | bytes 1179656 | tf_op jit(solution)/shard_map/ppermute | solution.py:18
  154.2 17.3 %copy-start.16 = (f32[128]{0:T(128)S(1)}, f32[128]{0:T(128)}, u32[]{:S(2)}) copy-start(f32[128]{0:T(128)} %param.21) | copy-start | bytes 1540
  173.7 39.3 %all-to-all-start.2 = ((bf16[8,4,256,128]{3,2,1,0:T(8,128)(2,1)}), bf16[8,4,256,128]{3,2,1,0:T(8,128)(2,1)}, u32[]{:S(2)}, u32[]{:S(2)}) async-start(bf16[8,4,256,128]{3,2,1,0:T(8,128)(2,1)} %broadcast_in_dim.62), calls=%async_computation.2 | async-start | bytes 4194304 | tf_op jit(solution)/shard_map/all_to_all | solution.py:43
  220.5 9.5 %all-to-all-start.3 = ((f32[8,3,1024]{2,1,0:T(4,128)}), f32[8,3,1024]{2,1,0:T(4,128)S(1)}, u32[]{:S(2)}, u32[]{:S(2)}) async-start(f32[8,3,1024]{2,1,0:T(4,128)} %broadcast_in_dim.64), calls=%async_computation.3 | async-start | bytes 262144 | tf_op jit(solution)/shard_map/all_to_all | solution.py:43
  (13 other events, 68.5 us)
